TPU v7x, 32 devices: a whole 2x2x4 slice. The times are simulated.
32 devices in a mesh: section: 2 (over x), dp: 8 (over z, y), tensor: 2 (over core).
Axes of the slice: x: 2, y: 2, z: 4, core: 2. Of those that a mesh axis runs over, the one named last changes fastest.
Arguments:
- images: bfloat16 [128, 196, 512], P('dp', 'tensor'), may hold values from -6 to 6
- cotangent: bfloat16 [128, 196, 512], P('dp', 'tensor'), may hold values from -6 to 6
- norm1_gain: bfloat16 [2, 512], P('section', 'dp'), may hold values from 0.5 to 1.5
- norm1_bias: bfloat16 [2, 512], P('section', 'dp'), may hold values from -1.75 to 1.75
- qkv_weight: bfloat16 [2, 512, 3, 512], P('section', 'dp', None, 'tensor'), may hold values from -0.25 to 0.25
- qkv_bias: bfloat16 [2, 3, 512], P('section', None, ('tensor', 'dp')), may hold values from -1.75 to 1.75
- position_table: float32 [2, 169, 16], P('section', None, 'tensor'), may hold values from -6 to 6
- proj_weight: bfloat16 [2, 512, 512], P('section', ('tensor', 'dp')), may hold values from -0.75 to 0.75
- proj_bias: bfloat16 [2, 512], P('section', 'dp'), may hold values from -1.75 to 1.75
- norm2_gain: bfloat16 [2, 512], P('section', 'dp'), may hold values from 0.5 to 1.5
- norm2_bias: bfloat16 [2, 512], P('section', 'dp'), may hold values from -1.75 to 1.75
- fc1_weight: bfloat16 [2, 512, 2048], P('section', 'dp', 'tensor'), may hold values from -0.25 to 0.25
- fc1_bias: bfloat16 [2, 2048], P('section', ('tensor', 'dp')), may hold values from -1.75 to 1.75
- fc2_weight: bfloat16 [2, 2048, 512], P('section', ('tensor', 'dp')), may hold values from -0.125 to 0.125
- fc2_bias: bfloat16 [2, 512], P('section', 'dp'), may hold values from -1.75 to 1.75
Outputs:
- activations: bfloat16 [2, 128, 196, 512], P('section', 'dp', 'tensor')
- input_grad: bfloat16 [2, 128, 196, 512], P('section', 'dp', 'tensor')
- norm1_gain_grad: float32 [2, 512], P('section', 'dp')
- norm1_bias_grad: float32 [2, 512], P('section', 'dp')
- qkv_weight_grad: float32 [2, 512, 3, 512], P('section', 'dp', None, 'tensor')
- qkv_bias_grad: float32 [2, 3, 512], P('section', None, ('tensor', 'dp'))
- position_table_grad: float32 [2, 169, 16], P('section', None, 'tensor')
- proj_weight_grad: float32 [2, 512, 512], P('section', ('tensor', 'dp'))
- proj_bias_grad: float32 [2, 512], P('section', 'dp')
- norm2_gain_grad: float32 [2, 512], P('section', 'dp')
- norm2_bias_grad: float32 [2, 512], P('section', 'dp')
- fc1_weight_grad: float32 [2, 512, 2048], P('section', 'dp', 'tensor')
- fc1_bias_grad: float32 [2, 2048], P('section', ('tensor', 'dp'))
- fc2_weight_grad: float32 [2, 2048, 512], P('section', ('tensor', 'dp'))
- fc2_bias_grad: float32 [2, 512], P('section', 'dp')
All inputs are finite; a program needn't handle non-finite values.
Results may differ from a plain program's by a relative error of at most 0.023.
Values may be sent and summed in bfloat16 or wider, within the bound.
A program may use at most 256 MiB of HBM per device.

v0:
```python
import jax
import jax.numpy as jnp
from jax import lax
from jax.sharding import PartitionSpec as P

D = 512
HEADS = 16
WIN = 7
SIDE = 14
SHIFT = 3
MICRO = 4
IMG_MB = 4


EPS = 1e-05
MASK_FILL = -100.0
ROOT_HALF = 0.7071067811865476
INV_ROOT_TWO_PI = 0.3989422804014327


def shifted(x, axis, by):
    size = lax.axis_size(axis)
    pairs = [(i, i + by) for i in range(size) if 0 <= i + by < size]
    return lax.ppermute(x, axis, pairs)


def to_windows(grid, shift_amount):
    image_count = grid.shape[0]
    channels = grid.shape[-1]
    across = SIDE // WIN
    spatial = grid.reshape(image_count, SIDE, SIDE, channels)
    spatial = jnp.roll(spatial, -shift_amount, 1)
    spatial = jnp.roll(spatial, -shift_amount, 2)
    spatial = spatial.reshape(image_count, across, WIN, across, WIN, channels).transpose(
        0, 1, 3, 2, 4, 5
    )
    return spatial.reshape(image_count, across * across, WIN * WIN, channels)


def from_windows(windowed, shift_amount):
    image_count = windowed.shape[0]
    channels = windowed.shape[-1]
    across = SIDE // WIN
    spatial = windowed.reshape(image_count, across, across, WIN, WIN, channels).transpose(
        0, 1, 3, 2, 4, 5
    )
    spatial = spatial.reshape(image_count, SIDE, SIDE, channels)
    spatial = jnp.roll(spatial, shift_amount, 1)
    spatial = jnp.roll(spatial, shift_amount, 2)
    return spatial.reshape(image_count, SIDE * SIDE, channels)


def relative_onehot():
    positions = jnp.arange(WIN * WIN)
    row_of = positions // WIN
    col_of = positions % WIN
    table_side = 2 * WIN - 1
    offsets = (row_of[:, None] - row_of[None, :] + WIN - 1) * table_side + (
        col_of[:, None] - col_of[None, :] + WIN - 1
    )
    return (offsets.reshape(-1)[:, None] == jnp.arange(table_side * table_side)[None, :]).astype(
        jnp.float32
    )


def region_mask(shift_amount, active):
    lines = jnp.arange(SIDE)
    region = jnp.where(lines < SIDE - WIN, 0, jnp.where(lines < SIDE - shift_amount, 1, 2))
    labels = (region[:, None] * 3 + region[None, :]).astype(jnp.float32)
    window_labels = to_windows(labels.reshape(1, SIDE * SIDE, 1), 0)[0, :, :, 0]
    differs = window_labels[:, :, None] != window_labels[:, None, :]
    return jnp.where(differs, MASK_FILL, 0.0).astype(jnp.float32) * active


def norm_stats(values):
    center = values - jnp.mean(values, -1, keepdims=True)
    inverse = lax.rsqrt(jnp.mean(center * center, -1, keepdims=True) + EPS)
    return (center * inverse, inverse)


def norm_backward(upstream, normed, inverse, gain):
    scaled = upstream * gain
    return inverse * (
        scaled
        - jnp.mean(scaled, -1, keepdims=True)
        - normed * jnp.mean(scaled * normed, -1, keepdims=True)
    )


def gelu_value(values):
    return 0.5 * values * (1.0 + jax.scipy.special.erf(values * ROOT_HALF))


def gelu_slope(values):
    return (
        0.5 * (1.0 + jax.scipy.special.erf(values * ROOT_HALF))
        + values * jnp.exp(-0.5 * values * values) * INV_ROOT_TWO_PI
    )


def gather_tokens(local_rows):
    return lax.all_gather(local_rows, "tensor", axis=1, tiled=True)


def scatter_tokens(partial_value):
    return lax.psum_scatter(
        partial_value.astype(jnp.bfloat16), "tensor", scatter_dimension=1, tiled=True
    ).astype(jnp.float32)


def gather_cotangent(local_rows):
    return lax.all_gather(local_rows, "tensor", axis=1, tiled=True)


def scatter_cotangent(partial_value):
    return lax.psum_scatter(
        partial_value.astype(jnp.bfloat16), "tensor", scatter_dimension=1, tiled=True
    ).astype(jnp.float32)


def per_device(
    images,
    cotangent,
    norm1_gain,
    norm1_bias,
    qkv_weight,
    qkv_bias,
    position_table,
    proj_weight,
    proj_bias,
    norm2_gain,
    norm2_bias,
    fc1_weight,
    fc1_bias,
    fc2_weight,
    fc2_bias,
):
    section = lax.axis_index("section")
    first_section = section == 0
    shift_amount = SHIFT * section
    active = section.astype(jnp.float32)
    gathered = (
        lax.all_gather(qkv_weight, "dp", axis=1, tiled=True),
        lax.all_gather(proj_weight, "dp", axis=1, tiled=True),
        lax.all_gather(fc1_weight, "dp", axis=1, tiled=True),
        lax.all_gather(fc2_weight, "dp", axis=1, tiled=True),
        lax.all_gather(qkv_bias, "dp", axis=2, tiled=True),
        lax.all_gather(fc1_bias, "dp", axis=1, tiled=True),
        lax.all_gather(norm1_gain, "dp", axis=1, tiled=True),
        lax.all_gather(norm1_bias, "dp", axis=1, tiled=True),
        lax.all_gather(proj_bias, "dp", axis=1, tiled=True),
        lax.all_gather(norm2_gain, "dp", axis=1, tiled=True),
        lax.all_gather(norm2_bias, "dp", axis=1, tiled=True),
        lax.all_gather(fc2_bias, "dp", axis=1, tiled=True),
    )
    (
        qkv_full,
        proj_full,
        fc1_full,
        fc2_full,
        qkv_bias_full,
        fc1_bias_full,
        gain_one,
        beta_one,
        proj_bias_full,
        gain_two,
        beta_two,
        fc2_bias_full,
    ) = [weight_piece[0] for weight_piece in gathered]
    table_local = position_table[0]
    qkv_bias_full = qkv_bias_full.astype(jnp.float32)
    fc1_bias_full = fc1_bias_full.astype(jnp.float32)
    gain_one = gain_one.astype(jnp.float32)
    beta_one = beta_one.astype(jnp.float32)
    proj_bias_full = proj_bias_full.astype(jnp.float32)
    gain_two = gain_two.astype(jnp.float32)
    beta_two = beta_two.astype(jnp.float32)
    fc2_bias_full = fc2_bias_full.astype(jnp.float32)
    onehot = relative_onehot()
    heads_local = table_local.shape[-1]
    head_size = D // HEADS
    scaling = head_size ** (-0.5)
    bias_flat = jnp.dot(onehot, table_local, precision=lax.Precision.HIGHEST)
    bias_heads = bias_flat.reshape(WIN * WIN, WIN * WIN, heads_local).transpose(2, 0, 1)
    window_mask = region_mask(shift_amount, active)

    def attention_scores(query_heads, key_heads):
        raw = jnp.einsum(
            "bwihd,bwjhd->bwhij", query_heads, key_heads, preferred_element_type=jnp.float32
        )
        return raw * scaling + bias_heads[None, None] + window_mask[None, :, None]

    local_rows = images.shape[1]
    batch_inputs = images.reshape(MICRO, IMG_MB, local_rows, D)
    batch_cotangents = cotangent.reshape(MICRO, IMG_MB, local_rows, D)
    incoming = jnp.zeros_like(batch_inputs[0])
    block_outputs = []
    stash = []
    for tick_index in range(MICRO + 1):
        source = jnp.where(first_section, batch_inputs[min(tick_index, MICRO - 1)], incoming)
        residual = source.astype(jnp.float32)
        forward_normed_one, forward_inverse_one = norm_stats(residual)
        first_norm = (forward_normed_one * gain_one + beta_one).astype(jnp.bfloat16)
        forward_windows_a = to_windows(gather_tokens(first_norm), shift_amount)
        projected = (
            jnp.einsum(
                "bwtc,cke->bwtke", forward_windows_a, qkv_full, preferred_element_type=jnp.float32
            )
            + qkv_bias_full
        )
        split_heads = projected.astype(jnp.bfloat16).reshape(
            projected.shape[:3] + (3, heads_local, head_size)
        )
        forward_query_heads = split_heads[:, :, :, 0]
        forward_key_heads = split_heads[:, :, :, 1]
        forward_value_heads = split_heads[:, :, :, 2]
        forward_scores = attention_scores(forward_query_heads, forward_key_heads)
        row_max = jnp.max(forward_scores, -1, keepdims=True)
        forward_log_total = row_max + jnp.log(
            jnp.sum(jnp.exp(forward_scores - row_max), -1, keepdims=True)
        )
        weights_b = jnp.exp(forward_scores - forward_log_total).astype(jnp.bfloat16)
        forward_context = jnp.einsum(
            "bwhij,bwjhd->bwihd", weights_b, forward_value_heads, preferred_element_type=jnp.float32
        ).astype(jnp.bfloat16)
        forward_context = forward_context.reshape(
            forward_context.shape[:3] + (heads_local * head_size,)
        )
        forward_partial_value = jnp.einsum(
            "bwte,ed->bwtd", forward_context, proj_full, preferred_element_type=jnp.float32
        )
        forward_midway = (
            residual
            + scatter_tokens(from_windows(forward_partial_value, shift_amount))
            + proj_bias_full
        )
        forward_normed_two, forward_inverse_two = norm_stats(forward_midway)
        second_norm = (forward_normed_two * gain_two + beta_two).astype(jnp.bfloat16)
        forward_mlp_rows = gather_tokens(second_norm)
        forward_hidden_pre = (
            jnp.einsum(
                "btc,cf->btf", forward_mlp_rows, fc1_full, preferred_element_type=jnp.float32
            )
            + fc1_bias_full
        )
        forward_activated = gelu_value(forward_hidden_pre).astype(jnp.bfloat16)
        mlp_out = jnp.einsum(
            "btf,fd->btd", forward_activated, fc2_full, preferred_element_type=jnp.float32
        )
        mlp_out = scatter_tokens(mlp_out)
        block_out = (forward_midway + mlp_out + fc2_bias_full).astype(jnp.bfloat16)
        forward_saved = (
            source,
            forward_windows_a,
            forward_query_heads,
            forward_key_heads,
            forward_value_heads,
            forward_log_total,
            forward_context,
            forward_midway,
            forward_mlp_rows,
            forward_hidden_pre,
        )
        block_out, saved = (block_out, forward_saved)
        block_outputs.append(block_out)
        stash.append(saved)
        if tick_index < MICRO:
            incoming = shifted(block_out, "section", 1)
    arriving = jnp.zeros_like(batch_cotangents[0])
    input_grads = []
    totals = None
    for tick_index in range(MICRO + 1):
        if tick_index < MICRO:
            from_output = batch_cotangents[MICRO - 1 - tick_index]
        else:
            from_output = jnp.zeros_like(batch_cotangents[0])
        grad_in = jnp.where(first_section, arriving, from_output)
        (
            block_in,
            windows_a,
            backward_query_heads,
            backward_key_heads,
            value_heads,
            log_total,
            context,
            midway,
            mlp_rows,
            hidden_pre,
        ) = stash[MICRO - tick_index]
        gradient = grad_in.astype(jnp.float32)
        fc2_bias_part = jnp.sum(gradient, (0, 1))
        grad_rows = gather_cotangent(grad_in)
        activated = gelu_value(hidden_pre).astype(jnp.bfloat16)
        fc2_part = jnp.einsum(
            "btf,btd->fd", activated, grad_rows, preferred_element_type=jnp.float32
        )
        hidden_grad = jnp.einsum(
            "btd,fd->btf", grad_rows, fc2_full, preferred_element_type=jnp.float32
        ) * gelu_slope(hidden_pre)
        fc1_bias_part = jnp.sum(hidden_grad, (0, 1))
        hidden_grad_b = hidden_grad.astype(jnp.bfloat16)
        fc1_part = jnp.einsum(
            "btc,btf->cf", mlp_rows, hidden_grad_b, preferred_element_type=jnp.float32
        )
        norm_two_grad = jnp.einsum(
            "btf,cf->btc", hidden_grad_b, fc1_full, preferred_element_type=jnp.float32
        )
        norm_two_grad = scatter_cotangent(norm_two_grad)
        normed_two, inverse_two = norm_stats(midway)
        midway_grad = gradient + norm_backward(norm_two_grad, normed_two, inverse_two, gain_two)
        gain_two_part = jnp.sum(norm_two_grad * normed_two, (0, 1))
        beta_two_part = jnp.sum(norm_two_grad, (0, 1))
        proj_bias_part = jnp.sum(midway_grad, (0, 1))
        midway_rows = to_windows(gather_cotangent(midway_grad.astype(jnp.bfloat16)), shift_amount)
        proj_part = jnp.einsum(
            "bwte,bwtd->ed", context, midway_rows, preferred_element_type=jnp.float32
        )
        context_grad = jnp.einsum(
            "bwtd,ed->bwte", midway_rows, proj_full, preferred_element_type=jnp.float32
        ).astype(jnp.bfloat16)
        context_grad = context_grad.reshape(backward_query_heads.shape)
        scores = attention_scores(backward_query_heads, backward_key_heads)
        soft = jnp.exp(scores - log_total)
        soft_b = soft.astype(jnp.bfloat16)
        prob_grad = jnp.einsum(
            "bwihd,bwjhd->bwhij", context_grad, value_heads, preferred_element_type=jnp.float32
        )
        value_grad = jnp.einsum(
            "bwhij,bwihd->bwjhd", soft_b, context_grad, preferred_element_type=jnp.float32
        )
        scores_grad = soft * (prob_grad - jnp.sum(soft * prob_grad, -1, keepdims=True))
        bias_part = jnp.sum(scores_grad, (0, 1))
        scores_b = scores_grad.astype(jnp.bfloat16)
        query_grad = (
            jnp.einsum(
                "bwhij,bwjhd->bwihd",
                scores_b,
                backward_key_heads,
                preferred_element_type=jnp.float32,
            )
            * scaling
        )
        key_grad = (
            jnp.einsum(
                "bwhij,bwihd->bwjhd",
                scores_b,
                backward_query_heads,
                preferred_element_type=jnp.float32,
            )
            * scaling
        )
        qkv_grad = jnp.stack([query_grad, key_grad, value_grad], 3).reshape(
            windows_a.shape[:3] + (3, heads_local * head_size)
        )
        qkv_bias_part = jnp.sum(qkv_grad, (0, 1, 2))
        qkv_grad_b = qkv_grad.astype(jnp.bfloat16)
        qkv_part = jnp.einsum(
            "bwtc,bwtke->cke", windows_a, qkv_grad_b, preferred_element_type=jnp.float32
        )
        norm_one_partial = jnp.einsum(
            "bwtke,cke->bwtc", qkv_grad_b, qkv_full, preferred_element_type=jnp.float32
        )
        norm_one_grad = scatter_cotangent(from_windows(norm_one_partial, shift_amount))
        normed_one, inverse_one = norm_stats(block_in.astype(jnp.float32))
        input_grad = (
            midway_grad + norm_backward(norm_one_grad, normed_one, inverse_one, gain_one)
        ).astype(jnp.bfloat16)
        gain_one_part = jnp.sum(norm_one_grad * normed_one, (0, 1))
        beta_one_part = jnp.sum(norm_one_grad, (0, 1))
        shared = jnp.stack(
            [
                gain_one_part,
                beta_one_part,
                proj_bias_part,
                gain_two_part,
                beta_two_part,
                fc2_bias_part,
            ]
        )
        input_grad, grad_terms = (
            input_grad,
            (
                qkv_part,
                proj_part,
                fc1_part,
                fc2_part,
                qkv_bias_part,
                fc1_bias_part,
                shared,
                bias_part,
            ),
        )
        input_grads.append(input_grad)
        totals = grad_terms if totals is None else jax.tree.map(jnp.add, totals, grad_terms)
        if tick_index < MICRO:
            arriving = shifted(input_grad, "section", -1)
    (
        qkv_total,
        proj_total,
        fc1_total,
        fc2_total,
        qkv_bias_total,
        fc1_bias_total,
        shared_total,
        bias_total,
    ) = totals
    table_part = jnp.dot(
        onehot.T,
        bias_total.transpose(1, 2, 0).reshape(-1, heads_local),
        precision=lax.Precision.HIGHEST,
    )
    reduced = (
        lax.psum_scatter(
            qkv_total.astype(jnp.bfloat16), "dp", scatter_dimension=0, tiled=True
        ).astype(jnp.float32),
        lax.psum_scatter(
            proj_total.astype(jnp.bfloat16), "dp", scatter_dimension=0, tiled=True
        ).astype(jnp.float32),
        lax.psum_scatter(
            fc1_total.astype(jnp.bfloat16), "dp", scatter_dimension=0, tiled=True
        ).astype(jnp.float32),
        lax.psum_scatter(
            fc2_total.astype(jnp.bfloat16), "dp", scatter_dimension=0, tiled=True
        ).astype(jnp.float32),
        lax.psum_scatter(
            qkv_bias_total.astype(jnp.bfloat16), "dp", scatter_dimension=1, tiled=True
        ).astype(jnp.float32),
        lax.psum_scatter(
            fc1_bias_total.astype(jnp.bfloat16), "dp", scatter_dimension=0, tiled=True
        ).astype(jnp.float32),
        lax.psum_scatter(
            shared_total.astype(jnp.bfloat16), "dp", scatter_dimension=1, tiled=True
        ).astype(jnp.float32),
    )
    shared_done = lax.psum(reduced[6], "tensor")
    table_done = lax.psum(table_part, "dp")
    activations = jnp.concatenate(
        [
            jnp.where(first_section, block_outputs[index_mb], block_outputs[index_mb + 1])
            for index_mb in range(MICRO)
        ],
        0,
    )
    input_grad_all = jnp.concatenate(
        [
            jnp.where(
                first_section, input_grads[MICRO - index_mb], input_grads[MICRO - 1 - index_mb]
            )
            for index_mb in range(MICRO)
        ],
        0,
    )
    return (
        activations[None],
        input_grad_all[None],
        shared_done[0][None],
        shared_done[1][None],
        reduced[0][None],
        reduced[4][None],
        table_done[None],
        reduced[1][None],
        shared_done[2][None],
        shared_done[3][None],
        shared_done[4][None],
        reduced[2][None],
        reduced[5][None],
        reduced[3][None],
        shared_done[5][None],
    )


def solution(mesh):
    in_specs = (
        P("dp", "tensor", None),
        P("dp", "tensor", None),
        P("section", "dp"),
        P("section", "dp"),
        P("section", "dp", None, "tensor"),
        P("section", None, ("tensor", "dp")),
        P("section", None, "tensor"),
        P("section", ("tensor", "dp"), None),
        P("section", "dp"),
        P("section", "dp"),
        P("section", "dp"),
        P("section", "dp", "tensor"),
        P("section", ("tensor", "dp")),
        P("section", ("tensor", "dp"), None),
        P("section", "dp"),
    )
    out_specs = (
        P("section", "dp", "tensor", None),
        P("section", "dp", "tensor", None),
        P("section", "dp"),
        P("section", "dp"),
        P("section", "dp", None, "tensor"),
        P("section", None, ("tensor", "dp")),
        P("section", None, "tensor"),
        P("section", ("tensor", "dp"), None),
        P("section", "dp"),
        P("section", "dp"),
        P("section", "dp"),
        P("section", "dp", "tensor"),
        P("section", ("tensor", "dp")),
        P("section", ("tensor", "dp"), None),
        P("section", "dp"),
    )
    return jax.shard_map(
        per_device, mesh=mesh, in_specs=in_specs, out_specs=out_specs, check_vma=False
    )
```

profile of v0, /device:TPU:0, one launch (start us, length us, event | category | flops | bytes accessed | tf_op | source)
XLA Modules:
  0.0 1549.2 jit_solution(6977974865451994998)
XLA Ops:
  8.9 32.3 %all_gather.100 = bf16[1,3,256]{1,0,2:T(2,128)(2,1)S(1)} all-gather(bf16[1,3,32]{1,0,2:T(2,128)(2,1)S(1)} %copy.281), channel_id=1, replica_groups=mesh['section'=2,'dp'=8,'tensor'=2] {'dp'}, dimensions={2}, use_global_device_ids=true | all-gather | bytes 1728 | tf_op jit(solution)/shard_map/all_gather | solution.py:147
  48.6 21.6 %all-reduce.27 = (bf16[512]{0:T(512)(128)(2,1)S(1)}, bf16[512]{0:T(512)(128)(2,1)S(1)}, bf16[512]{0:T(512)(128)(2,1)S(1)}, bf16[512]{0:T(512)(128)(2,1)S(1)}, bf...) all-reduce(bf16[512]{0:T(512)(128)(2,1)S(1)} %dynamic-update-slice., ...), channel_id=1, replica_groups=mesh['section'=2,'dp'=8,'tensor'=2] {'dp'}, use_global_device_ids=true, to_apply=%add.3 | all-reduce | flops 3072 | bytes 12288
  79.8 32.5 %all_gather.99 = bf16[1,512,3,256]{3,1,2,0:T(8,128)(2,1)S(1)} all-gather(bf16[1,64,3,256]{3,1,2,0:T(8,128)(2,1)S(1)} %copy-done.207), channel_id=1, replica_groups=mesh['section'=2,'dp'=8,'tensor'=2] {'dp'}, dimensions={1}, use_global_device_ids=true | all-gather | bytes 884736 | tf_op jit(solution)/shard_map/all_gather | solution.py:143
  131.3 30.7 %all_gather.101 = bf16[1,256,512]{2,1,0:T(8,128)(2,1)S(1)} all-gather(bf16[1,32,512]{2,1,0:T(8,128)(2,1)S(1)} %copy-done.215), channel_id=1, replica_groups=mesh['section'=2,'dp'=8,'tensor'=2] {'dp'}, dimensions={1}, use_global_device_ids=true | all-gather | bytes 294912 | tf_op jit(solution)/shard_map/all_gather | solution.py:144
  168.1 16.5 %all_gather.107 = bf16[1,1024]{1,0:T(2,128)(2,1)S(1)} all-gather(bf16[1,128]{1,0:T(2,128)(2,1)S(1)} %copy-done.249), channel_id=1, replica_groups=mesh['section'=2,'dp'=8,'tensor'=2] {'dp'}, dimensions={1}, use_global_device_ids=true | all-gather | bytes 2304 | tf_op jit(solution)/shard_map/all_gather | solution.py:148
  193.0 14.1 all-gather.3.cloned.1.call-done
  211.3 36.8 %all-gather.5.cloned.1.call-done = bf16[1,1024,512]{2,1,0:T(8,128)(2,1)} async-done(((bf16[1,128,512]{2,1,0:T(8,128)(2,1)}), bf16[1,1024,512]{2,1,0:T(8,128)(2,1)}) %all-gather.5.cloned.1.call-update) | async-done | bytes 1048592 | tf_op jit(solution)/shard_map/all_gather | solution.py:146
  252.3 17.8 %all-reduce.51.cloned.1.call-done = bf16[4,196,512]{2,0,1:T(4,128)(2,1)} async-done(((bf16[4,196,512]{2,0,1:T(4,128)(2,1)}), bf16[4,196,512]{2,0,1:T(4,128)(2,1)}) %all-reduce.51.cloned.1.call-update) | async-done | bytes 802832
  309.9 20.6 %all-reduce.53.cloned.1.call-done = bf16[4,196,512]{2,0,1:T(4,128)(2,1)} async-done(((bf16[4,196,512]{2,0,1:T(4,128)(2,1)}), bf16[4,196,512]{2,0,1:T(4,128)(2,1)}) %all-reduce.53.cloned.1.call-update) | async-done | bytes 802832
  344.5 20.3 %all-reduce.55.cloned.1.call-done = bf16[4,196,512]{2,0,1:T(4,128)(2,1)} async-done(((bf16[4,196,512]{2,0,1:T(4,128)(2,1)}), bf16[4,196,512]{2,0,1:T(4,128)(2,1)}) %all-reduce.55.cloned.1.call-update) | async-done | bytes 802832
  411.8 20.9 %all-reduce.57.cloned.1.call-done = bf16[4,196,512]{2,0,1:T(4,128)(2,1)} async-done(((bf16[4,196,512]{2,0,1:T(4,128)(2,1)}), bf16[4,196,512]{2,0,1:T(4,128)(2,1)}) %all-reduce.57.cloned.1.call-update) | async-done | bytes 802832
  444.9 20.3 %all-reduce.59.cloned.1.call-done = bf16[4,196,512]{2,0,1:T(4,128)(2,1)} async-done(((bf16[4,196,512]{2,0,1:T(4,128)(2,1)}), bf16[4,196,512]{2,0,1:T(4,128)(2,1)}) %all-reduce.59.cloned.1.call-update) | async-done | bytes 802832
  512.4 20.6 %all-reduce.61.cloned.1.call-done = bf16[4,196,512]{2,0,1:T(4,128)(2,1)} async-done(((bf16[4,196,512]{2,0,1:T(4,128)(2,1)}), bf16[4,196,512]{2,0,1:T(4,128)(2,1)}) %all-reduce.61.cloned.1.call-update) | async-done | bytes 802832
  545.4 20.3 %all-reduce.63.cloned.1.call-done = bf16[4,196,512]{2,0,1:T(4,128)(2,1)} async-done(((bf16[4,196,512]{2,0,1:T(4,128)(2,1)}), bf16[4,196,512]{2,0,1:T(4,128)(2,1)}) %all-reduce.63.cloned.1.call-update) | async-done | bytes 802832
  611.2 16.2 %all-reduce.65.cloned.1.call-done = bf16[4,196,512]{2,0,1:T(4,128)(2,1)} async-done(((bf16[4,196,512]{2,0,1:T(4,128)(2,1)}), bf16[4,196,512]{2,0,1:T(4,128)(2,1)}) %all-reduce.65.cloned.1.call-update) | async-done | bytes 802832
  643.9 20.3 %all-reduce.67.cloned.1.call-done = bf16[4,196,512]{2,0,1:T(4,128)(2,1)} async-done(((bf16[4,196,512]{2,0,1:T(4,128)(2,1)}), bf16[4,196,512]{2,0,1:T(4,128)(2,1)}) %all-reduce.67.cloned.1.call-update) | async-done | bytes 802832
  707.8 20.3 %all-reduce.69.cloned.1.call-done = bf16[4,196,512]{2,0,1:T(4,128)(2,1)} async-done(((bf16[4,196,512]{2,0,1:T(4,128)(2,1)}), bf16[4,196,512]{2,0,1:T(4,128)(2,1)}) %all-reduce.69.cloned.1.call-update) | async-done | bytes 802832
  733.9 12.0 collective-permute-done.4
  757.2 19.4 %all-reduce.71.cloned.1.call-done = bf16[4,196,512]{2,0,1:T(4,128)(2,1)} async-done(((bf16[4,196,512]{2,0,1:T(4,128)(2,1)}), bf16[4,196,512]{2,0,1:T(4,128)(2,1)}) %all-reduce.71.cloned.1.call-update) | async-done | bytes 802832
  820.3 20.3 %all-reduce.73.cloned.1.call-done = bf16[4,196,512]{2,0,1:T(4,128)(2,1)} async-done(((bf16[4,196,512]{2,0,1:T(4,128)(2,1)}), bf16[4,196,512]{2,0,1:T(4,128)(2,1)}) %all-reduce.73.cloned.1.call-update) | async-done | bytes 802832
  869.3 19.4 %all-reduce.75.cloned.1.call-done = bf16[4,196,512]{2,0,1:T(4,128)(2,1)} async-done(((bf16[4,196,512]{2,0,1:T(4,128)(2,1)}), bf16[4,196,512]{2,0,1:T(4,128)(2,1)}) %all-reduce.75.cloned.1.call-update) | async-done | bytes 802832
  929.8 20.3 %all-reduce.77.cloned.1.call-done = bf16[4,196,512]{2,0,1:T(4,128)(2,1)} async-done(((bf16[4,196,512]{2,0,1:T(4,128)(2,1)}), bf16[4,196,512]{2,0,1:T(4,128)(2,1)}) %all-reduce.77.cloned.1.call-update) | async-done | bytes 802832
  982.8 15.2 all-reduce.79.cloned.1.call-done
  1045.5 12.6 all-reduce.81.cloned.1.call-done
  1093.1 12.9 all-reduce.83.cloned.1.call-done
  1183.3 21.8 %all-reduce.26 = bf16[1024]{0:T(1024)(128)(2,1)S(1)} all-reduce(bf16[1024]{0:T(1024)(128)(2,1)S(1)} %add_convert_fusion.16), channel_id=27, replica_groups=mesh['section'=2,'dp'=8,'tensor'=2] {'dp'}, use_global_device_ids=true, to_apply=%region_127.132.clone | all-reduce | flops 1024 | bytes 4096
  1215.0 18.1 %psum.15 = f32[1,169,8]{1,2,0:T(8,128)} all-reduce(f32[1,169,8]{1,2,0:T(8,128)S(1)} %fusion.92), channel_id=1, replica_groups=mesh['section'=2,'dp'=8,'tensor'=2] {'dp'}, use_global_device_ids=true, to_apply=%region_119.124 | all-reduce | flops 1352 | bytes 10816 | tf_op jit(solution)/shard_map/psum | solution.py:436
  1234.5 35.8 %reduce-scatter.13.cloned.1.call-done = bf16[32,512]{1,0:T(8,128)(2,1)} async-done(((bf16[256,512]{1,0:T(8,128)(2,1)}), bf16[32,512]{1,0:T(8,128)(2,1)}) %reduce-scatter.13.cloned.1.call-update) | async-done | bytes 32784 | tf_op jit(solution)/shard_map/reduce_scatter | solution.py:416
  1271.7 65.9 %reduce-scatter.15.cloned.1.call-done = bf16[64,1024]{1,0:T(8,128)(2,1)} async-done(((bf16[512,1024]{1,0:T(8,128)(2,1)}), bf16[64,1024]{1,0:T(8,128)(2,1)}) %reduce-scatter.15.cloned.1.call-update) | async-done | bytes 131088 | tf_op jit(solution)/shard_map/reduce_scatter | solution.py:419
  1339.3 65.7 %reduce-scatter.17.cloned.1.call-done = bf16[128,512]{1,0:T(8,128)(2,1)} async-done(((bf16[1024,512]{1,0:T(8,128)(2,1)}), bf16[128,512]{1,0:T(8,128)(2,1)}) %reduce-scatter.17.cloned.1.call-update) | async-done | bytes 131088 | tf_op jit(solution)/shard_map/reduce_scatter | solution.py:422
  1406.6 64.4 %reduce-scatter.11.cloned.1.call-done = bf16[64,3,256]{2,0,1:T(8,128)(2,1)} async-done(((bf16[512,3,256]{2,0,1:T(8,128)(2,1)}), bf16[64,3,256]{2,0,1:T(8,128)(2,1)}) %reduce-scatter.11.cloned.1.call-update) | async-done | bytes 98320 | tf_op jit(solution)/shard_map/reduce_scatter | solution.py:413
  1484.7 53.4 %reduce-scatter.19.cloned.1.call-done = bf16[64,6]{1,0:T(8,128)(2,1)} async-done(((bf16[512,6]{1,0:T(8,128)(2,1)}), bf16[64,6]{1,0:T(8,128)(2,1)}) %reduce-scatter.19.cloned.1.call-update) | async-done | bytes 784
  (1046 shorter events, 687.9 us)
Async XLA Ops:
  8.0 177.9 %all-reduce.49.cloned.1.call-start = ((), (), s32[]{:S(2)}) async-start(), calls=%async_computation.14 | async-start | bytes 1605632
  166.9 40.2 %all-gather.3.cloned.1.call-start = ((), (), s32[]{:S(2)}) async-start(), calls=%async_computation.6 | async-start | bytes 1179648 | tf_op jit(solution)/shard_map/all_gather | solution.py:145
  167.5 80.6 %all-gather.5.cloned.1.call-start = ((), (), s32[]{:S(2)}) async-start(), calls=%async_computation.7 | async-start | bytes 1179648 | tf_op jit(solution)/shard_map/all_gather | solution.py:146
  168.1 102.0 %all-reduce.51.cloned.1.call-start = ((), (), s32[]{:S(2)}) async-start(), calls=%async_computation.15 | async-start | bytes 1605632
  252.2 78.3 %all-reduce.53.cloned.1.call-start = ((), (), s32[]{:S(2)}) async-start(), calls=%async_computation.16 | async-start | bytes 1605632
  309.4 55.4 %all-reduce.55.cloned.1.call-start = ((), (), s32[]{:S(2)}) async-start(), calls=%async_computation.17 | async-start | bytes 1605632
  344.4 88.2 %all-reduce.57.cloned.1.call-start = ((), (), s32[]{:S(2)}) async-start(), calls=%async_computation.18 | async-start | bytes 1605632
  367.2 12.7 collective-permute-start.1
  411.6 53.7 %all-reduce.59.cloned.1.call-start = ((), (), s32[]{:S(2)}) async-start(), calls=%async_computation.19 | async-start | bytes 1605632
  444.9 88.2 %all-reduce.61.cloned.1.call-start = ((), (), s32[]{:S(2)}) async-start(), calls=%async_computation.20 | async-start | bytes 1605632
  512.0 53.7 %all-reduce.63.cloned.1.call-start = ((), (), s32[]{:S(2)}) async-start(), calls=%async_computation.21 | async-start | bytes 1605632
  545.4 82.1 %all-reduce.65.cloned.1.call-start = ((), (), s32[]{:S(2)}) async-start(), calls=%async_computation.22 | async-start | bytes 1605632
  606.3 57.8 %all-reduce.67.cloned.1.call-start = ((), (), s32[]{:S(2)}) async-start(), calls=%async_computation.23 | async-start | bytes 1605632
  643.8 84.3 %all-reduce.69.cloned.1.call-start = ((), (), s32[]{:S(2)}) async-start(), calls=%async_computation.24 | async-start | bytes 1605632
  707.7 68.9 %all-reduce.71.cloned.1.call-start = ((), (), s32[]{:S(2)}) async-start(), calls=%async_computation.25 | async-start | bytes 1605632
  732.6 13.3 collective-permute-start.4
  757.1 83.5 %all-reduce.73.cloned.1.call-start = ((), (), s32[]{:S(2)}) async-start(), calls=%async_computation.26 | async-start | bytes 1605632
  820.3 68.4 %all-reduce.75.cloned.1.call-start = ((), (), s32[]{:S(2)}) async-start(), calls=%async_computation.27 | async-start | bytes 1605632
  846.0 13.3 collective-permute-start.5
  869.2 80.9 %all-reduce.77.cloned.1.call-start = ((), (), s32[]{:S(2)}) async-start(), calls=%async_computation.28 | async-start | bytes 1605632
  929.8 68.3 %all-reduce.79.cloned.1.call-start = ((), (), s32[]{:S(2)}) async-start(), calls=%async_computation.29 | async-start | bytes 1605632
  955.5 13.3 collective-permute-start.6
  978.6 79.5 %all-reduce.81.cloned.1.call-start = ((), (), s32[]{:S(2)}) async-start(), calls=%async_computation.30 | async-start | bytes 1605632
  1037.8 68.3 %all-reduce.83.cloned.1.call-start = ((), (), s32[]{:S(2)}) async-start(), calls=%async_computation.31 | async-start | bytes 1605632
  1063.5 13.5 collective-permute-start.7
  1086.6 146.6 %reduce-scatter.21.cloned.1.call-start = ((), (), s32[]{:S(2)}) async-start(), calls=%async_computation.13 | async-start | bytes 73728
  1141.4 128.9 %reduce-scatter.13.cloned.1.call-start = ((), (), s32[]{:S(2)}) async-start(), calls=%async_computation.9 | async-start | bytes 294912 | tf_op jit(solution)/shard_map/reduce_scatter | solution.py:416
  1146.6 191.1 %reduce-scatter.15.cloned.1.call-start = ((), (), s32[]{:S(2)}) async-start(), calls=%async_computation.10 | async-start | bytes 1179648 | tf_op jit(solution)/shard_map/reduce_scatter | solution.py:419
  1153.6 251.4 %reduce-scatter.17.cloned.1.call-start = ((), (), s32[]{:S(2)}) async-start(), calls=%async_computation.11 | async-start | bytes 1179648 | tf_op jit(solution)/shard_map/reduce_scatter | solution.py:422
  1164.1 306.9 %reduce-scatter.11.cloned.1.call-start = ((), (), s32[]{:S(2)}) async-start(), calls=%async_computation.8 | async-start | bytes 884736 | tf_op jit(solution)/shard_map/reduce_scatter | solution.py:413
  1175.5 297.2 %all-reduce.85.cloned.1.call-start = ((), (), s32[]{:S(2)}) async-start(), calls=%async_computation.32 | async-start | bytes 3211264
  1213.1 325.0 %reduce-scatter.19.cloned.1.call-start = ((), (), s32[]{:S(2)}) async-start(), calls=%async_computation.12 | async-start | bytes 147456
  (285 other events, 4725.5 us)
Sparse Core Ops, SparseCore 0:
  167.0 16.2 all-reduce.48
  252.3 17.7 all-reduce.50
  309.5 20.9 all-reduce.52
  344.6 20.2 all-reduce.54
  411.7 20.9 all-reduce.56
  445.0 20.2 all-reduce.58
  512.1 20.9 all-reduce.60
  545.5 20.2 all-reduce.62
  606.5 20.9 all-reduce.64
  643.9 20.2 all-reduce.66
  707.8 20.2 all-reduce.68
  757.2 19.3 all-reduce.70
  820.4 20.2 all-reduce.72
  869.3 19.3 all-reduce.74
  929.9 20.2 all-reduce.76
  978.7 19.3 all-reduce.78
  1037.9 20.2 all-reduce.80
  1086.7 19.2 all-reduce.82
  1213.2 17.7 all-reduce.84
Sparse Core Ops, SparseCore 1:
  169.5 37.6 all-gather.2
  209.1 38.9 all-gather.4
  1141.5 63.7 reduce-scatter.20
  1209.1 61.1 reduce-scatter.12
  1274.3 63.3 reduce-scatter.14
  1341.7 63.3 reduce-scatter.16
  1408.2 62.8 reduce-scatter.10
  1477.2 60.9 reduce-scatter.18
where the time goes:
time: 1560 us; the launch traced here: 1550 us
  waiting for transfers between devices  736 us (47%)
  blocking collectives  225 us (14%)
  matrix products  197 us (13%)
  other arithmetic  194 us (12%)
  local copies, waits for them, and re-layouts  153 us (10%)
  starting transfers between devices  22.9 us (1%)
  between operations  21.4 us (1%)
    unnamed x48, waiting for transfers between devices  373 us
    ppermute x8, waiting for transfers between devices, shifted(): return lax.ppermute(x, axis, pairs)  79.8 us
    reduce_scatter x1, waiting for transfers between devices, per_device(): lax.psum_scatter(fc1_total.astype(jnp.bfloat16), 'dp', scatter_dimension=...  65.9 us
    reduce_scatter x1, waiting for transfers between devices, per_device(): lax.psum_scatter(fc2_total.astype(jnp.bfloat16), 'dp', scatter_dimension=...  65.7 us
    reduce_scatter x1, waiting for transfers between devices, per_device(): lax.psum_scatter(qkv_total.astype(jnp.bfloat16), 'dp', scatter_dimension=...  64.4 us
    unnamed x2, blocking collectives  43.4 us
    another operation x15, local copies, waits for them, and re-layouts, per_device(): jnp.stack([query_grad, key_grad, value_grad], 3)  41.6 us
    all_gather x1, waiting for transfers between devices, per_device(): lax.all_gather(fc2_weight, 'dp', axis=1, tiled=True)  36.8 us
  transfers between devices with their start and end apart: 35, of which 32 were waited for; matrix products, arithmetic and copies ran while one was open for 6% of the time, Pallas kernels for 0%

commit v1 on v0

v1 whole, which is shorter than its diff:
```python
import functools
import math
import types

import jax
import jax.numpy as jnp
import numpy as np
from jax import lax
from jax.experimental import pallas as pl
from jax.experimental.pallas import tpu as pltpu
from jax.sharding import PartitionSpec as P

HEADS = 16
WIN = 7
SIDE = 14
SHIFT = 3

EPS = 1e-05
MASK_FILL = -100.0
ROOT_HALF = 0.7071067811865476
INV_ROOT_TWO_PI = 0.3989422804014327

ACROSS = SIDE // WIN
NW = ACROSS * ACROSS
WT = WIN * WIN
WP = 64
TABLE_SIDE = 2 * WIN - 1
CENTER = (WIN - 1) * TABLE_SIDE + WIN - 1
TABLE_PAD = 256
CH = 512
GATHER_ROWS = 16

SECTION = "section"
DP = "dp"
TENSOR = "tensor"

f32 = jnp.float32
bf16 = jnp.bfloat16
MESH = pl.DeviceIdType.MESH
NN = ((1,), (0,))
NT = ((1,), (1,))
TN = ((0,), (0,))


def round_up(n, m):
    return -(-n // m) * m


def window_slots(shift):
    slot = np.zeros(SIDE * SIDE, np.int64)
    for p in range(SIDE):
        for q in range(SIDE):
            token = ((p + shift) % SIDE) * SIDE + (q + shift) % SIDE
            window = (p // WIN) * ACROSS + q // WIN
            slot[token] = window * WP + (p % WIN) * WIN + q % WIN
    return slot


def window_permutation(parts, half, padded):
    perm = np.zeros((2, NW * WP, parts * padded), np.float32)
    for block in range(2):
        for token, slot in enumerate(window_slots(SHIFT * block)):
            perm[block, slot, (token // half) * padded + token % half] = 1
    return perm


def dotf(a, b, dims):
    return lax.dot_general(a, b, (dims, ((), ())), preferred_element_type=f32)


def normalize(values):
    center = values - jnp.mean(values, -1, keepdims=True)
    inverse = lax.rsqrt(jnp.mean(center * center, -1, keepdims=True) + EPS)
    return center * inverse, inverse


def norm_pull(upstream, normed, inverse, gain):
    scaled = upstream * gain
    return inverse * (
        scaled
        - jnp.mean(scaled, -1, keepdims=True)
        - normed * jnp.mean(scaled * normed, -1, keepdims=True)
    )


def block(i, n):
    if isinstance(i, int):
        return pl.ds(i * n, n)
    return pl.ds(pl.multiple_of(i * n, n), n)


def column_sum(v):
    return jnp.sum(v, 0, keepdims=True)


class Sizes:
    def __init__(self, mesh, images, fc1_weight):
        self.sections = mesh.shape[SECTION]
        self.dp = mesh.shape[DP]
        self.parts = mesh.shape[TENSOR]
        inner = int(math.isqrt(self.dp))
        while self.dp % inner:
            inner -= 1
        self.nb = inner
        self.na = self.dp // inner
        self.local_images, self.half, self.d = images.shape
        self.ff = fc1_weight.shape[-1] * self.parts
        self.ni = self.local_images // (self.sections * self.parts)
        self.hp = round_up(self.half, 8)
        self.rows = self.parts * self.hp
        self.m = self.ni * self.rows
        self.mw = self.ni * NW * WP
        self.hd = self.d // HEADS
        self.quad = 128 // self.hd
        self.ng = HEADS // self.quad
        self.nch = self.ff // CH
        self.scaling = self.hd**-0.5
        self.heads_part = HEADS // self.parts


QKV, PROJ, FC1, FC2, SMALL = range(5)
KINDS = (SMALL, QKV, PROJ, FC1, FC2)


def kernel(z, *refs):
    names = z.names
    r = types.SimpleNamespace(**dict(zip(names, refs)))
    s = lax.axis_index(SECTION)
    d = lax.axis_index(DP)
    t = lax.axis_index(TENSOR)
    na, nb, nt, ns, ni = z.na, z.nb, z.parts, z.sections, z.ni
    a = d // nb
    b = lax.rem(d, nb)
    rows, m = z.rows, z.m

    def dev(s_=None, a_=None, b_=None, t_=None):
        s_ = s if s_ is None else s_
        a_ = a if a_ is None else a_
        b_ = b if b_ is None else b_
        t_ = t if t_ is None else t_
        return (s_, a_ * nb + b_, t_)

    def off(base, k, n):
        return lax.rem(base + k, n)

    x_peers = [off(s, k, ns) for k in range(1, ns)]
    a_peers = [off(a, k, na) for k in range(1, na)]
    a_from = [off(a, na - k, na) for k in range(1, na)]
    b_peers = [off(b, k, nb) for k in range(1, nb)]
    b_from = [off(b, nb - k, nb) for k in range(1, nb)]
    c_peers = [off(t, k, nt) for k in range(1, nt)]
    c_from = [off(t, nt - k, nt) for k in range(1, nt)]
    x_from = [off(s, ns - k, ns) for k in range(1, ns)]

    def part(p, n):
        return pl.ds(pl.multiple_of(p * n, 128), n)

    def win(w, ref, lead, a_, b_, t_):
        if w == QKV:
            return ref.at[lead + (slice(None), a_, b_, slice(None), part(t_, z.d // nt))]
        if w == FC1:
            return ref.at[lead + (a_, b_, slice(None), part(t_, z.ff // nt))]
        return ref.at[lead + (t_, a_, b_)]

    ALL = slice(None)
    wref = {QKV: r.wq, PROJ: r.wp, FC1: r.w1, FC2: r.w2, SMALL: r.sm}
    own = {QKV: r.q_in, PROJ: r.p_in, FC1: r.f1_in, FC2: r.f2_in, SMALL: r.sm_in}
    lx, xs = r.lx, r.xs
    zs, zr, ys, yr, cs, cr = r.zs, r.zr, r.ys, r.yr, r.cs, r.cr

    def remote(src, dst, ss, rs, device):
        return pltpu.make_async_remote_copy(
            src_ref=src, dst_ref=dst, send_sem=ss, recv_sem=rs, device_id=device, device_id_type=MESH
        )

    sends = []

    def send(src, dst, ss, rs, device):
        c = remote(src, dst, ss, rs, device)
        c.start()
        sends.append(c)

    def arrived(dst, sem):
        pltpu.make_async_copy(dst, dst, sem).wait()

    def start_x(w):
        target = win(w, wref[w], (s,), a, b, t)
        pltpu.make_async_copy(own[w], target, lx.at[w, s]).start()
        for k, peer in enumerate(x_peers):
            send(own[w], target, xs.at[w, k], lx.at[w, s], dev(s_=peer))

    def go_z(w, p):
        here = win(w, wref[w], (p,), a, b, t)
        arrived(here, lx.at[w, p])
        for k, peer in enumerate(a_peers):
            send(here, here, zs.at[w, p, k], zr.at[w, p, k], dev(a_=peer))

    def go_y(w, p):
        for k, source in enumerate(a_from):
            arrived(win(w, wref[w], (p,), source, b, t), zr.at[w, p, k])
        here = win(w, wref[w], (p,), ALL, b, t)
        for k, peer in enumerate(b_peers):
            send(here, here, ys.at[w, p, k], yr.at[w, p, k], dev(b_=peer))

    def go_c(w, p):
        for k, source in enumerate(b_from):
            arrived(win(w, wref[w], (p,), ALL, source, t), yr.at[w, p, k])
        here = win(w, wref[w], (p,), ALL, ALL, t)
        for k, peer in enumerate(c_peers):
            send(here, here, cs.at[w, p, k], cr.at[w, p, k], dev(t_=peer))

    def ready(w, p):
        for k, source in enumerate(c_from):
            arrived(win(w, wref[w], (p,), ALL, ALL, source), cr.at[w, p, k])

    group = s * nt + t

    def group_images(g):
        return pl.ds(g * ni, ni)

    barrier = pltpu.get_barrier_semaphore()
    peers = (
        [dev(a_=p) for p in a_peers]
        + [dev(b_=p) for p in b_peers]
        + [dev(t_=p) for p in c_peers]
        + [dev(s_=p) for p in x_peers]
        + [dev(s_=p, t_=q) for p in x_peers for q in c_peers]
    )
    for p in peers:
        pl.semaphore_signal(barrier, inc=1, device_id=p, device_id_type=MESH)
    pl.semaphore_wait(barrier, len(peers))

    for w in KINDS:
        start_x(w)
    tbl = r.tbl
    pltpu.make_async_copy(r.tbl_in, tbl.at[s, t], r.tx.at[s]).start()
    for k, peer in enumerate(x_peers):
        send(r.tbl_in, tbl.at[s, t], r.txs.at[k], r.tx.at[s], dev(s_=peer))
    xin = r.outb
    for j, src in enumerate((r.images, r.cotangent)):
        pltpu.make_async_copy(src.at[group_images(group)], xin.at[j, t], r.xl.at[j]).start()
        for k, peer in enumerate(c_peers):
            send(
                src.at[group_images(s * nt + peer)],
                xin.at[j, t],
                r.xcs.at[j, k],
                r.xcr.at[j, k],
                dev(t_=peer),
            )

    def image_ready(j):
        arrived(xin.at[j, t], r.xl.at[j])
        for k, source in enumerate(c_from):
            arrived(xin.at[j, source], r.xcr.at[j, k])

    pad_rows = jnp.zeros((z.hp - z.half, z.d), f32)

    def load_rows(j, ref):
        def one(i, _):
            pieces = []
            for h in range(nt):
                pieces.append(xin[j, h, i].astype(f32))
                if z.hp > z.half:
                    pieces.append(pad_rows)
            ref[block(i, rows), :] = jnp.concatenate(pieces, 0).astype(bf16)
            return 0

        lax.fori_loop(0, ni, one, 0)

    outb = r.outb

    def ship(kind, p, slot):
        out = r.act if kind == 0 else r.ig
        for h in range(nt):
            target = out.at[group_images(group)]
            mine = jnp.logical_and(s == p, t == h)

            @pl.when(mine)
            def _():
                pltpu.make_async_copy(outb.at[slot, h], target, r.os.at[kind, p, h]).start()

            @pl.when(jnp.logical_not(mine))
            def _():
                remote(
                    outb.at[slot, h], target, r.os.at[kind, p, h], r.orr.at[kind, group], (p, d, h)
                ).start()

    def shipped(kind, p, slot):
        for h in range(nt):
            arrived(outb.at[slot, h], r.os.at[kind, p, h])

    def received(kind):
        out = r.act if kind == 0 else r.ig
        for g in range(ns * nt):

            @pl.when(g != group)
            def _():
                arrived(out.at[group_images(g)], r.orr.at[kind, g])

    def stage_out(value, i, slot):
        for h in range(nt):
            outb[slot, h, i] = value[h * z.hp : h * z.hp + z.half].astype(bf16)

    def w_qkv(p, c):
        return r.wq[p, c].reshape(z.d, z.d)

    def w_proj(p):
        return r.wp[p].reshape(z.d, z.d)

    def w_fc1(p, c):
        return r.w1[p, :, :, :, block(c, CH)].reshape(z.d, CH)

    w2_per = CH // r.w2.shape[-2]
    w2_all = r.w2.reshape(2, z.nch, w2_per, r.w2.shape[-2], z.d)

    def w_fc2(p, c):
        return w2_all[p, c].reshape(CH, z.d)

    SMF = r.smf

    def unpack_small(p):
        acc = jnp.zeros((GATHER_ROWS, z.d), f32)
        for t_ in range(nt):
            for a_ in range(na):
                for b_ in range(nb):
                    acc = acc + r.sm[p, t_, a_, b_].astype(f32)
        SMF[p] = acc

    def row(p, k):
        return SMF[p, pl.ds(k, 1), :]

    def masks(dtype):
        lane = lax.broadcasted_iota(jnp.int32, (WP, 128), 1) // z.hd
        return [(lane == h).astype(dtype) for h in range(z.quad)]

    def spread(v, mk):
        return jnp.concatenate([v * q for q in mk], 0)

    def collect(v, mk):
        acc = v[0:WP] * mk[0]
        for h in range(1, z.quad):
            acc = acc + v[h * WP : (h + 1) * WP] * mk[h]
        return acc

    BM = r.bm
    lanes = 128
    per_lane = lanes // WP

    def build_bias(p):
        j = lax.broadcasted_iota(jnp.int32, (WP, lanes), 0)
        lane = lax.broadcasted_iota(jnp.int32, (WP, lanes), 1)
        i = lax.rem(lane, WP)
        iy, ix, jy, jx = i // WIN, lax.rem(i, WIN), j // WIN, lax.rem(j, WIN)
        valid = jnp.logical_and(i < WT, j < WT)
        index = (iy - jy + WIN - 1) * TABLE_SIDE + ix - jx + WIN - 1
        index = jnp.where(valid, index, 0)
        low = jnp.where(index < lanes, index, 0)
        high = jnp.where(index < lanes, 0, index - lanes)
        head_of_lane = lane // WP

        def look(head):
            tt, hh = head // z.heads_part, head % z.heads_part
            entry = tbl[p, tt, pl.ds(hh, 1), :]
            one = jnp.take_along_axis(jnp.broadcast_to(entry[:, :lanes], (WP, lanes)), low, axis=1)
            two = jnp.take_along_axis(jnp.broadcast_to(entry[:, lanes:], (WP, lanes)), high, axis=1)
            return jnp.where(index < lanes, one, two)

        def region(q, wy):
            first = jnp.zeros_like(q)
            if wy < ACROSS - 1:
                return first
            return jnp.where(q < WIN - SHIFT, first + 1, first + 2)

        for g in range(z.ng):
            for c in range(z.quad // per_lane):
                value = look(g * z.quad + c * per_lane)
                for e in range(1, per_lane):
                    value = jnp.where(head_of_lane == e, look(g * z.quad + c * per_lane + e), value)
                value = jnp.where(j < WT, value, -1e30)
                for w in range(NW if p else 1):
                    out = value
                    if p == 1:
                        wy, wx = w // ACROSS, w % ACROSS
                        label_i = region(iy, wy) * 3 + region(ix, wx)
                        label_j = region(jy, wy) * 3 + region(jx, wx)
                        out = out + jnp.where(
                            jnp.logical_and(valid, label_i != label_j), MASK_FILL, 0.0
                        )
                    BM[p + w, g, :, c * lanes : (c + 1) * lanes] = out

    X, G = r.x, r.g
    PM, PMT = r.pm, r.pmt
    FN, N1, K = r.fn, r.n1, r.k
    QK, PR, CTX, CTXT = r.qk, r.pr, r.ctx, r.ctxt
    MID, MG, SN, N2, ACT, SL = r.mid, r.mg, r.sn, r.n2, r.actv, r.sl
    SG, DB = r.sg, r.db

    def forward(p, hook):
        def ln1(i, _):
            n, inv = normalize(X[block(i, rows), :].astype(f32))
            N1[p, block(i, rows), :] = n.astype(bf16)
            K[block(i, rows), 2 * p : 2 * p + 1] = inv
            f = (n * row(p, 0) + row(p, 1)).astype(bf16)
            FN[p, block(i, rows), :] = f
            CTX[block(i, NW * WP), :] = dotf(PM[p], f, NN).astype(bf16)
            return 0

        hook("ln1")
        lax.fori_loop(0, ni, ln1, 0)
        hook("qkv")

        def qkv(c, _):
            QK[p, c] = (dotf(CTX[...], w_qkv(p, c), NN) + row(p, 6 + c)).astype(bf16)
            return 0

        lax.fori_loop(0, 3, qkv, 0)

        def attention(u, _):
            mb, mf = masks(bf16), masks(f32)
            w = 1 + lax.rem(u, NW) if p else 0
            for g in range(z.ng):
                L = slice(g * 128, (g + 1) * 128)
                q = QK[p, 0, block(u, WP), L]
                k = QK[p, 1, block(u, WP), L]
                v = QK[p, 2, block(u, WP), L]
                sc = dotf(k, spread(q, mb), NT) * z.scaling + BM[w, g]
                e = jnp.exp(sc - jnp.max(sc, 0, keepdims=True))
                pr = (e * (1.0 / jnp.sum(e, 0, keepdims=True))).astype(bf16)
                PR[p, u, g] = pr
                CTX[block(u, WP), L] = collect(dotf(pr, v, TN), mf).astype(bf16)
            return 0

        steps = ni * NW
        hook("attn0")
        lax.fori_loop(0, steps // 2, attention, 0)
        hook("attn1")
        lax.fori_loop(steps // 2, steps, attention, 0)

        def unperm(i, _):
            CTXT[p, block(i, rows), :] = dotf(PMT[p], CTX[block(i, NW * WP), :], NN).astype(bf16)
            return 0

        lax.fori_loop(0, ni, unperm, 0)
        hook("proj")
        MID[...] = dotf(CTXT[p], w_proj(p), NN)

        def ln2(i, _):
            mid = X[block(i, rows), :].astype(f32) + MID[block(i, rows), :] + row(p, 2)
            MID[block(i, rows), :] = mid
            n, inv = normalize(mid)
            N2[p, block(i, rows), :] = n.astype(bf16)
            K[block(i, rows), 2 * p + 1 : 2 * p + 2] = inv
            SN[p, block(i, rows), :] = (n * row(p, 3) + row(p, 4)).astype(bf16)
            return 0

        lax.fori_loop(0, ni, ln2, 0)
        hook("fc1")

        def rise(c, _):
            u = dotf(SN[p], w_fc1(p, c), NN) + row(p, 9 + c)
            e = 0.5 * (1.0 + lax.erf(u * ROOT_HALF))
            ACT[c] = (u * e).astype(bf16)
            SL[c] = (e + u * jnp.exp(-0.5 * u * u) * INV_ROOT_TWO_PI).astype(bf16)
            return 0

        lax.fori_loop(0, z.nch, rise, 0)
        hook("fc2")

        def fall(c, _):
            MID[...] += dotf(ACT[c], w_fc2(p, c), NN)
            return 0

        lax.fori_loop(0, z.nch, fall, 0)
        hook("out")

        def finish(i, _):
            value = MID[block(i, rows), :] + row(p, 5)
            X[block(i, rows), :] = value.astype(bf16)
            stage_out(value, i, p % 2)
            return 0

        lax.fori_loop(0, ni, finish, 0)
        ship(0, p, p % 2)

    gq, gp, g1, g2 = r.gq, r.gp, r.g1, r.g2
    g2_all = g2.reshape(z.nch, w2_per, g2.shape[-2], z.d)

    def backward(p, hook):
        def addrow(k, v):
            SG[p, pl.ds(k, 1), 0 : z.d] = SG[p, pl.ds(k, 1), 0 : z.d] + v

        SG[p] = jnp.zeros(SG.shape[1:], f32)
        DB[...] = jnp.zeros(DB.shape, f32)

        hook("fc2")

        def fc2(c, _):
            g2_all[c] = dotf(ACT[c], G[...], TN).astype(bf16).reshape(g2_all.shape[1:])
            hg = dotf(G[...], w_fc2(p, c), NT) * SL[c].astype(f32)
            SG[p, pl.ds(9 + c, 1), 0 : z.d] = column_sum(hg)
            SL[c] = hg.astype(bf16)
            return 0

        lax.fori_loop(0, z.nch, fc2, 0)
        hook("fc1")

        def fc1(c, _):
            g1[:, :, :, block(c, CH)] = (
                dotf(SN[p], SL[c], TN).astype(bf16).reshape(g1.shape[:-1] + (CH,))
            )
            return 0

        lax.fori_loop(0, z.nch, fc1, 0)
        hook("n2g")
        MID[...] = dotf(SL[0], w_fc1(p, 0), NT)

        def n2g(c, _):
            MID[...] += dotf(SL[c], w_fc1(p, c), NT)
            return 0

        lax.fori_loop(1, z.nch, n2g, 0)

        def ln2(i, _):
            sl = block(i, rows)
            ng = MID[sl, :]
            n = N2[p, sl, :].astype(f32)
            g = G[sl, :].astype(f32)
            mg = g + norm_pull(ng, n, K[sl, 2 * p + 1 : 2 * p + 2], row(p, 3))
            MG[sl, :] = mg
            addrow(5, column_sum(g))
            addrow(3, column_sum(ng * n))
            addrow(4, column_sum(ng))
            addrow(2, column_sum(mg))
            G[sl, :] = mg.astype(bf16)
            return 0

        lax.fori_loop(0, ni, ln2, 0)
        hook("proj")
        gp[...] = dotf(CTXT[p], G[...], TN).astype(bf16).reshape(gp.shape)
        CTXT[p] = dotf(G[...], w_proj(p), NT).astype(bf16)

        def cgrad(i, _):
            CTX[block(i, NW * WP), :] = dotf(PM[p], CTXT[p, block(i, rows), :], NN).astype(bf16)
            return 0

        lax.fori_loop(0, ni, cgrad, 0)

        def attention(u, _):
            mb, mf = masks(bf16), masks(f32)
            for g in range(z.ng):
                L = slice(g * 128, (g + 1) * 128)
                q = QK[p, 0, block(u, WP), L]
                k = QK[p, 1, block(u, WP), L]
                v = QK[p, 2, block(u, WP), L]
                pr = PR[p, u, g]
                cbd = spread(CTX[block(u, WP), L], mb)
                qbd = spread(q, mb)
                pf = pr.astype(f32)
                tt = pf * dotf(v, cbd, NT)
                sc = tt - pf * jnp.sum(tt, 0, keepdims=True)
                DB[g] = DB[g] + sc
                sb = sc.astype(bf16)
                QK[p, 1, block(u, WP), L] = (dotf(sb, qbd, NN) * z.scaling).astype(bf16)
                QK[p, 2, block(u, WP), L] = dotf(pr, cbd, NN).astype(bf16)
                QK[p, 0, block(u, WP), L] = (collect(dotf(sb, k, TN), mf) * z.scaling).astype(bf16)
            return 0

        steps = ni * NW
        hook("attn0")
        lax.fori_loop(0, steps // 2, attention, 0)
        hook("attn1")
        lax.fori_loop(steps // 2, steps, attention, 0)
        hook("qkv")
        for c in range(3):

            def un(i, _):
                dv = dotf(PMT[p], QK[p, c, block(i, NW * WP), :], NN)
                addrow(6 + c, column_sum(dv))
                QK[p, c, block(i, rows), :] = dv.astype(bf16)
                return 0

            lax.fori_loop(0, ni, un, 0)
            gq[c] = dotf(FN[p], QK[p, c, 0:m, :], TN).astype(bf16).reshape(gq.shape[1:])
        hook("qkv_done")
        for c in range(3):
            v = dotf(QK[p, c, 0:m, :], w_qkv(p, c), NT)
            MID[...] = v if c == 0 else MID[...] + v
        hook("ln1")

        def ln1(i, _):
            sl = block(i, rows)
            ng = MID[sl, :]
            n = N1[p, sl, :].astype(f32)
            xg = MG[sl, :] + norm_pull(ng, n, K[sl, 2 * p : 2 * p + 1], row(p, 0))
            addrow(0, column_sum(ng * n))
            addrow(1, column_sum(ng))
            G[sl, :] = xg.astype(bf16)
            stage_out(xg, i, 1 - p)
            return 0

        lax.fori_loop(0, ni, ln1, 0)
        ship(1, p, 1 - p)
        table_rows(p)

    def table_rows(p):
        src = lax.broadcasted_iota(jnp.int32, (z.quad * WP, TABLE_PAD), 0)
        dst = lax.broadcasted_iota(jnp.int32, (z.quad * WP, TABLE_PAD), 1)
        i = lax.rem(src, WP)
        place = jnp.logical_and(
            i < WT, dst == CENTER - ((i // WIN) * TABLE_SIDE + lax.rem(i, WIN))
        )
        head = src // WP
        j = lax.broadcasted_iota(jnp.int32, (WP, TABLE_PAD), 0)
        jy = j // WIN
        step = TABLE_SIDE - WIN
        for h in range(z.quad):
            pick = jnp.logical_and(place, head == h).astype(bf16)
            for g in range(z.ng):
                v = DB[g]
                hi = v.astype(bf16)
                lo = (v - hi.astype(f32)).astype(bf16)
                e = dotf(hi, pick, NN) + dotf(lo, pick, NN)
                e = pltpu.roll(e, 0, 1, stride=1, stride_axis=0)
                for bit in (1, 2, 4):
                    moved = pltpu.roll(e, step * bit, 1)
                    e = jnp.where(lax.rem(jy // bit, 2) == 1, moved, e)
                e = jnp.where(j < WT, e, 0.0)
                SG[p, pl.ds(g * z.quad + h, 1), z.d :] = column_sum(e)

    gref = {QKV: gq, PROJ: gp, FC1: g1, FC2: g2}
    rx1 = {QKV: r.q1, PROJ: r.p1, FC1: r.f11, FC2: r.f21}
    rx2 = {QKV: r.q2, PROJ: r.p2, FC1: r.f12, FC2: r.f22}
    rx3 = {QKV: r.q3, PROJ: r.p3, FC1: r.f13, FC2: r.f23}
    rx4 = {QKV: r.q4, PROJ: r.p4, FC1: r.f14, FC2: r.f24}
    gout = {QKV: r.gq_out, PROJ: r.gp_out, FC1: r.g1_out, FC2: r.g2_out}
    s1, v1, s2, v2, s3, v3, s4, v4 = (r.s1, r.v1, r.s2, r.v2, r.s3, r.v3, r.s4, r.v4)
    k1, k2, k3 = r.k1, r.k2, r.k3

    def credit(sem, w, k, p, device):
        if p == 1:
            pl.semaphore_signal(sem.at[w, k], inc=1, device_id=device, device_id_type=MESH)

    def spend(sem, w, k, p):
        if p == 0:
            pl.semaphore_wait(sem.at[w, k], 1)

    def r1(w, p):
        for k, peer in enumerate(c_peers):
            spend(k1, w, k, p)
            remote(
                win(w, gref[w], (), ALL, ALL, peer), rx1[w].at[k], s1.at[w, k], v1.at[w, k], dev(t_=peer)
            ).start()

    def r2(w, p):
        mine = win(w, gref[w], (), ALL, ALL, t)
        for k, source in enumerate(c_from):
            arrived(rx1[w].at[k], v1.at[w, k])
        add_into(w, mine, [rx1[w].at[k] for k in range(nt - 1)])
        for k, source in enumerate(c_from):
            credit(k1, w, k, p, dev(t_=source))
        for k, peer in enumerate(b_peers):
            spend(k2, w, k, p)
            remote(
                win(w, gref[w], (), ALL, peer, t), rx2[w].at[k], s2.at[w, k], v2.at[w, k], dev(b_=peer)
            ).start()

    def r3(w, p):
        mine = win(w, gref[w], (), ALL, b, t)
        for k, source in enumerate(b_from):
            arrived(rx2[w].at[k], v2.at[w, k])
        add_into(w, mine, [rx2[w].at[k] for k in range(nb - 1)])
        for k, source in enumerate(b_from):
            credit(k2, w, k, p, dev(b_=source))
        for k, peer in enumerate(a_peers):
            spend(k3, w, k, p)
            remote(
                win(w, gref[w], (), peer, b, t), rx3[w].at[k], s3.at[w, k], v3.at[w, k], dev(a_=peer)
            ).start()

    def r4(w, p):
        mine = win(w, gref[w], (), a, b, t)
        for k, source in enumerate(a_from):
            arrived(rx3[w].at[k], v3.at[w, k])
        total = mine[...].astype(f32)
        for k in range(na - 1):
            total = total + rx3[w][k].astype(f32)
        for k, source in enumerate(a_from):
            credit(k3, w, k, p, dev(a_=source))

        @pl.when(s == p)
        def _():
            gout[w][...] = total

        @pl.when(s != p)
        def _():
            mine[...] = total.astype(bf16)
            remote(mine, rx4[w], s4.at[w], v4.at[w], dev(s_=p)).start()

    def r5(w, p):
        @pl.when(s == p)
        def _():
            arrived(rx4[w], v4.at[w])
            gout[w][...] = gout[w][...] + rx4[w][...].astype(f32)

        @pl.when(s != p)
        def _():
            arrived(win(w, gref[w], (), a, b, t), s4.at[w])

        for k, peer in enumerate(c_peers):
            arrived(win(w, gref[w], (), ALL, ALL, peer), s1.at[w, k])
        for k, peer in enumerate(b_peers):
            arrived(win(w, gref[w], (), ALL, peer, t), s2.at[w, k])
        for k, peer in enumerate(a_peers):
            arrived(win(w, gref[w], (), peer, b, t), s3.at[w, k])

    def add_into(w, mine, others):
        lead = mine.shape[:-2]
        count = int(np.prod(lead))

        def one(i, _):
            index = []
            rest = i
            for extent in reversed(lead):
                index.append(lax.rem(rest, extent))
                rest = rest // extent
            index = tuple(reversed(index))
            total = mine[index].astype(f32)
            for o in others:
                total = total + o[index].astype(f32)
            mine[index] = total.astype(bf16)
            return 0

        lax.fori_loop(0, count, one, 0)

    for w in KINDS:
        go_z(w, 0)
    for q in range(ns):
        arrived(tbl.at[q, t], r.tx.at[q])
        for k, peer in enumerate(c_peers):
            send(tbl.at[q, t], tbl.at[q, t], r.tcs.at[q, k], r.tcr.at[q, k], dev(t_=peer))
    image_ready(0)
    load_rows(0, X)
    for q in range(ns):
        for k, source in enumerate(c_from):
            arrived(tbl.at[q, source], r.tcr.at[q, k])
    for p in range(2):
        build_bias(p)
    for w in (SMALL, QKV):
        go_y(w, 0)
    for w in (SMALL, QKV):
        go_c(w, 0)
    image_ready(1)
    load_rows(1, G)

    def forward_hook(p, name):
        if p == 0:
            if name == "ln1":
                ready(SMALL, 0)
                unpack_small(0)
                go_z(SMALL, 1)
            if name == "qkv":
                ready(QKV, 0)
            if name == "attn0":
                go_y(PROJ, 0)
                go_y(FC1, 0)
                go_c(PROJ, 0)
            if name == "attn1":
                go_c(FC1, 0)
                go_y(FC2, 0)
                for w in (QKV, PROJ, FC1, FC2):
                    go_z(w, 1)
            if name == "proj":
                ready(PROJ, 0)
                go_c(FC2, 0)
                go_y(SMALL, 1)
                go_c(SMALL, 1)
            if name == "fc1":
                ready(FC1, 0)
            if name == "fc2":
                go_y(QKV, 1)
                ready(FC2, 0)
            if name == "out":
                go_c(QKV, 1)
                for j, ref in enumerate((ACT, SL)):
                    pltpu.make_async_copy(ref, r.spill.at[j], r.sp.at[j]).start()
        else:
            if name == "ln1":
                ready(SMALL, 1)
                unpack_small(1)
            if name == "qkv":
                ready(QKV, 1)
                go_y(PROJ, 1)
            if name == "attn0":
                go_c(PROJ, 1)
                go_y(FC1, 1)
            if name == "attn1":
                go_c(FC1, 1)
                go_y(FC2, 1)
            if name == "proj":
                ready(PROJ, 1)
                go_c(FC2, 1)
            if name == "fc1":
                for j, ref in enumerate((ACT, SL)):
                    arrived(ref, r.sp.at[j])
                ready(FC1, 1)
            if name == "fc2":
                ready(FC2, 1)

    for p in range(2):
        forward(p, functools.partial(forward_hook, p))

    def backward_hook(p, name):
        if p == 1:
            if name == "fc2":
                shipped(0, 0, 0)
            if name == "fc1":
                r1(FC2, 1)
            if name == "n2g":
                r1(FC1, 1)
                r2(FC2, 1)
            if name == "proj":
                for j, ref in enumerate((ACT, SL)):
                    pltpu.make_async_copy(r.spill.at[j], ref, r.sp.at[j]).start()
            if name == "attn0":
                r1(PROJ, 1)
                r2(FC1, 1)
            if name == "attn1":
                r3(FC2, 1)
                r2(PROJ, 1)
            if name == "qkv":
                r3(FC1, 1)
                r3(PROJ, 1)
                r4(FC2, 1)
            if name == "qkv_done":
                r1(QKV, 1)
                r4(FC1, 1)
                r4(PROJ, 1)
            if name == "ln1":
                r2(QKV, 1)
                r5(FC2, 1)
                r5(FC1, 1)
        else:
            if name == "fc2":
                shipped(0, 1, 1)
                for j, ref in enumerate((ACT, SL)):
                    arrived(ref, r.sp.at[j])
            if name == "fc1":
                r1(FC2, 0)
                r3(QKV, 1)
                r5(PROJ, 1)
            if name == "n2g":
                r1(FC1, 0)
                r2(FC2, 0)
                r4(QKV, 1)
            if name == "attn0":
                r1(PROJ, 0)
                r2(FC1, 0)
                r5(QKV, 1)
            if name == "attn1":
                r3(FC2, 0)
                r2(PROJ, 0)
            if name == "qkv":
                r3(FC1, 0)
                r3(PROJ, 0)
                r4(FC2, 0)
            if name == "qkv_done":
                r1(QKV, 0)
                r4(FC1, 0)
                r4(PROJ, 0)
            if name == "ln1":
                r2(QKV, 0)
                r5(FC2, 0)
                r5(FC1, 0)
                r5(PROJ, 0)

    for p in (1, 0):
        backward(p, functools.partial(backward_hook, p))

    ra, rb, rc, rd = r.ra, r.rb, r.rc, r.rd
    ss, sv = r.ss, r.sv
    slots = iter(range(16))

    def exchange(src, dst, targets, sources):
        ids = [next(slots) for _ in targets]
        for k, target in enumerate(targets):
            send(src(k), dst.at[k], ss.at[ids[k]], sv.at[ids[k]], target)
        for k in range(len(sources)):
            arrived(dst.at[k], sv.at[ids[k]])

    exchange(lambda k: SG, ra, [dev(t_=p) for p in c_peers], c_from)
    r.sum1[...] = SG[...] + sum(ra[k] for k in range(nt - 1))
    r3(QKV, 0)
    exchange(lambda k: r.sum1.at[x_peers[k]], rb, [dev(s_=p) for p in x_peers], x_from)
    r.sum2[...] = r.sum1[s] + sum(rb[k] for k in range(ns - 1))
    exchange(lambda k: r.sum2, rc, [dev(b_=p) for p in b_peers], b_from)
    r.sum3[...] = r.sum2[...] + sum(rc[k] for k in range(nb - 1))
    exchange(lambda k: r.sum3, rd, [dev(a_=p) for p in a_peers], a_from)
    r4(QKV, 0)
    r.small_out[...] = r.sum3[...] + sum(rd[k] for k in range(na - 1))
    r5(QKV, 0)

    received(0)
    received(1)
    shipped(1, 1, 0)
    shipped(1, 0, 1)
    for c in sends:
        c.wait_send()


def per_device(z, images, cotangent, norm1_gain, norm1_bias, qkv_weight, qkv_bias, position_table,
               proj_weight, proj_bias, norm2_gain, norm2_bias, fc1_weight, fc1_bias, fc2_weight,
               fc2_bias):
    s = lax.axis_index(SECTION)
    d = lax.axis_index(DP)
    t = lax.axis_index(TENSOR)
    D, nt, na, nb, ns, ni = z.d, z.parts, z.na, z.nb, z.sections, z.ni
    part = t * z.dp + d

    def spread_to(values, width, at):
        blank = jnp.zeros((values.shape[0], width), bf16)
        return lax.dynamic_update_slice(blank, values, (0, at))

    vectors = jnp.concatenate(
        [norm1_gain, norm1_bias, proj_bias, norm2_gain, norm2_bias, fc2_bias], 0
    )
    vectors = jnp.where(t == 0, vectors, jnp.zeros_like(vectors))
    small = jnp.concatenate(
        [
            spread_to(vectors, D, d * vectors.shape[1]),
            spread_to(qkv_bias[0], D, part * qkv_bias.shape[-1]),
            spread_to(fc1_bias, z.ff, part * fc1_bias.shape[-1]).reshape(-1, D),
        ],
        0,
    )
    small = jnp.pad(small, ((0, GATHER_ROWS - small.shape[0]), (0, 0)))
    table = jnp.pad(position_table[0].T, ((0, 0), (0, TABLE_PAD - position_table.shape[1])))
    perm = window_permutation(nt, z.half, z.hp)

    qrow, prow, f2row = qkv_weight.shape[1], proj_weight.shape[1], fc2_weight.shape[1]
    m, mw, nch = z.m, z.mw, z.nch
    S = jax.ShapeDtypeStruct
    V = pl.BlockSpec(memory_space=pltpu.VMEM)
    A = pl.BlockSpec(memory_space=pl.ANY)
    dma = pltpu.SemaphoreType.DMA
    reg = pltpu.SemaphoreType.REGULAR
    inputs = dict(
        images=(images, A),
        cotangent=(cotangent, A),
        q_in=(qkv_weight[0].transpose(1, 0, 2), A),
        p_in=(proj_weight[0], A),
        f1_in=(fc1_weight[0], A),
        f2_in=(fc2_weight[0], A),
        sm_in=(small, V),
        tbl_in=(table, V),
        pm=(jnp.asarray(perm, bf16), V),
        pmt=(jnp.asarray(perm.transpose(0, 2, 1), bf16), V),
    )
    wide = D + TABLE_PAD
    outputs = dict(
        act=(S(images.shape, bf16), A),
        ig=(S(images.shape, bf16), A),
        gq_out=(S((3, qrow, D // nt), f32), V),
        gp_out=(S((prow, D), f32), V),
        g1_out=(S((qrow, z.ff // nt), f32), V),
        g2_out=(S((f2row, D), f32), V),
        small_out=(S((GATHER_ROWS, wide), f32), V),
        spill=(S((2, nch, m, CH), bf16), A),
    )
    vm = pltpu.VMEM
    W = 5
    scratch = dict(
        wq=vm((2, 3, na, nb, qrow, D), bf16),
        wp=vm((2, nt, na, nb, prow, D), bf16),
        w1=vm((2, na, nb, qrow, z.ff), bf16),
        w2=vm((2, nt, na, nb, f2row, D), bf16),
        sm=vm((2, nt, na, nb, GATHER_ROWS, D), bf16),
        smf=vm((2, GATHER_ROWS, D), f32),
        tbl=vm((2, nt, z.heads_part, TABLE_PAD), f32),
        outb=vm((2, nt, ni, z.half, D), bf16),
        bm=vm((1 + NW, z.ng, WP, z.quad * WP), f32),
        x=vm((m, D), bf16),
        g=vm((m, D), bf16),
        fn=vm((2, m, D), bf16),
        n1=vm((2, m, D), bf16),
        k=vm((m, 4), f32),
        qk=vm((2, 3, mw, D), bf16),
        pr=vm((2, ni * NW, z.ng, WP, z.quad * WP), bf16),
        ctx=vm((mw, D), bf16),
        ctxt=vm((2, m, D), bf16),
        mid=vm((m, D), f32),
        mg=vm((m, D), f32),
        sn=vm((2, m, D), bf16),
        n2=vm((2, m, D), bf16),
        actv=vm((nch, m, CH), bf16),
        sl=vm((nch, m, CH), bf16),
        sg=vm((2, GATHER_ROWS, wide), f32),
        db=vm((z.ng, WP, z.quad * WP), f32),
        gq=vm((3, na, nb, qrow, D), bf16),
        gp=vm((nt, na, nb, prow, D), bf16),
        g1=vm((na, nb, qrow, z.ff), bf16),
        g2=vm((nt, na, nb, f2row, D), bf16),
        q1=vm((nt - 1, 3, na, nb, qrow, D // nt), bf16),
        p1=vm((nt - 1, na, nb, prow, D), bf16),
        f11=vm((nt - 1, na, nb, qrow, z.ff // nt), bf16),
        f21=vm((nt - 1, na, nb, f2row, D), bf16),
        q2=vm((nb - 1, 3, na, qrow, D // nt), bf16),
        p2=vm((nb - 1, na, prow, D), bf16),
        f12=vm((nb - 1, na, qrow, z.ff // nt), bf16),
        f22=vm((nb - 1, na, f2row, D), bf16),
        q3=vm((na - 1, 3, qrow, D // nt), bf16),
        p3=vm((na - 1, prow, D), bf16),
        f13=vm((na - 1, qrow, z.ff // nt), bf16),
        f23=vm((na - 1, f2row, D), bf16),
        q4=vm((3, qrow, D // nt), bf16),
        p4=vm((prow, D), bf16),
        f14=vm((qrow, z.ff // nt), bf16),
        f24=vm((f2row, D), bf16),
        ra=vm((nt - 1, 2, GATHER_ROWS, wide), f32),
        rb=vm((ns - 1, GATHER_ROWS, wide), f32),
        rc=vm((nb - 1, GATHER_ROWS, wide), f32),
        rd=vm((na - 1, GATHER_ROWS, wide), f32),
        sum1=vm((2, GATHER_ROWS, wide), f32),
        sum2=vm((GATHER_ROWS, wide), f32),
        sum3=vm((GATHER_ROWS, wide), f32),
        lx=dma((W, ns)),
        xs=dma((W, ns - 1)),
        zs=dma((W, 2, na - 1)),
        zr=dma((W, 2, na - 1)),
        ys=dma((W, 2, nb - 1)),
        yr=dma((W, 2, nb - 1)),
        cs=dma((W, 2, nt - 1)),
        cr=dma((W, 2, nt - 1)),
        tx=dma((ns,)),
        txs=dma((ns - 1,)),
        tcs=dma((ns, nt - 1)),
        tcr=dma((ns, nt - 1)),
        xl=dma((2,)),
        xcs=dma((2, nt - 1)),
        xcr=dma((2, nt - 1)),
        os=dma((2, 2, nt)),
        orr=dma((2, ns * nt)),
        sp=dma((2,)),
        s1=dma((4, nt - 1)),
        v1=dma((4, nt - 1)),
        s2=dma((4, nb - 1)),
        v2=dma((4, nb - 1)),
        s3=dma((4, na - 1)),
        v3=dma((4, na - 1)),
        s4=dma((4,)),
        v4=dma((4,)),
        k1=reg((4, nt - 1)),
        k2=reg((4, nb - 1)),
        k3=reg((4, na - 1)),
        ss=dma((16,)),
        sv=dma((16,)),
    )
    z.names = list(inputs) + list(outputs) + list(scratch)
    results = pl.pallas_call(
        functools.partial(kernel, z),
        out_shape=tuple(o for o, _ in outputs.values()),
        in_specs=[spec for _, spec in inputs.values()],
        out_specs=tuple(spec for _, spec in outputs.values()),
        scratch_shapes=list(scratch.values()),
        compiler_params=pltpu.CompilerParams(
            collective_id=0, has_side_effects=True, vmem_limit_bytes=67043328
        ),
        name="two_blocks",
    )(*[x for x, _ in inputs.values()])
    act, ig, gq, gp, g1, g2, sums, _ = results

    def own_vector(k):
        width = norm1_gain.shape[1]
        return lax.dynamic_slice(sums, (k, d * width), (1, width))

    width = qkv_bias.shape[-1]
    qkv_bias_grad = lax.dynamic_slice(sums, (6, part * width), (3, width))[None]
    width = fc1_bias.shape[1]
    fc1_flat = sums[9 : 9 + nch, :D].reshape(1, -1)
    fc1_bias_grad = lax.dynamic_slice(fc1_flat, (0, part * width), (1, width))
    tables = lax.dynamic_slice(sums, (t * z.heads_part, D), (z.heads_part, TABLE_PAD))
    tables = tables[:, : position_table.shape[1]][:, ::-1].T[None]
    return (
        act[None],
        ig[None],
        own_vector(0),
        own_vector(1),
        gq.transpose(1, 0, 2)[None],
        qkv_bias_grad,
        tables,
        gp[None],
        own_vector(2),
        own_vector(3),
        own_vector(4),
        g1[None],
        fc1_bias_grad,
        g2[None],
        own_vector(5),
    )


def solution(mesh):
    def run(*args):
        z = Sizes(mesh, args[0], args[11])
        return per_device(z, *args)

    in_specs = (
        P(DP, TENSOR, None),
        P(DP, TENSOR, None),
        P(SECTION, DP),
        P(SECTION, DP),
        P(SECTION, DP, None, TENSOR),
        P(SECTION, None, (TENSOR, DP)),
        P(SECTION, None, TENSOR),
        P(SECTION, (TENSOR, DP), None),
        P(SECTION, DP),
        P(SECTION, DP),
        P(SECTION, DP),
        P(SECTION, DP, TENSOR),
        P(SECTION, (TENSOR, DP)),
        P(SECTION, (TENSOR, DP), None),
        P(SECTION, DP),
    )
    out_specs = (
        P(SECTION, DP, TENSOR, None),
        P(SECTION, DP, TENSOR, None),
        P(SECTION, DP),
        P(SECTION, DP),
        P(SECTION, DP, None, TENSOR),
        P(SECTION, None, (TENSOR, DP)),
        P(SECTION, None, TENSOR),
        P(SECTION, (TENSOR, DP), None),
        P(SECTION, DP),
        P(SECTION, DP),
        P(SECTION, DP),
        P(SECTION, DP, TENSOR),
        P(SECTION, (TENSOR, DP)),
        P(SECTION, (TENSOR, DP), None),
        P(SECTION, DP),
    )
    return jax.shard_map(
        run, mesh=mesh, in_specs=in_specs, out_specs=out_specs, check_vma=False
    )
```

time: 1560 us -> 290 us (0.19)
  waiting for transfers between devices: 736 us -> 0 us
  Pallas kernels: 0 us -> 265 us
  blocking collectives: 225 us -> 0 us
  matrix products: 197 us -> 0 us
  other arithmetic: 194 us -> 0.66 us
  local copies, waits for them, and re-layouts: 153 us -> 22.7 us
  starting transfers between devices: 22.9 us -> 0 us
  between operations: 21.4 us -> 0.73 us
    unnamed x48 -> x0, waiting for transfers between devices: 373 us -> none
    pallas_call x0 -> x1, Pallas kernels: none -> 265 us  [per_device(): pl.pallas_call(functools.partial(kernel, z), out_shape=tuple((o for o, _...]
    reduce_scatter x4 -> x0, waiting for transfers between devices: 232 us -> none  [the longest x1 65.9 us: per_device(): lax.psum_scatter(fc1_total.astype(jnp.bfloat16), 'dp', scatter_dimension=...]
    dot_general x92 -> x0, matrix products: 197 us -> none  [the longest x5 23.1 us: per_device(): jnp.einsum('bwhij,bwihd->bwjhd', soft_b, context_grad, preferred_element_...]
    all_gather x24 -> x0, blocking collectives: 161 us -> none  [the longest x1 32.5 us: per_device(): lax.all_gather(qkv_weight, 'dp', axis=1, tiled=True)]
    reduce_sum x55 -> x0, other arithmetic: 88.9 us -> none  [the longest x5 13.7 us: per_device(): gain_two_part = jnp.sum(norm_two_grad * normed_two, (0, 1))]
    ppermute x8 -> x0, waiting for transfers between devices: 79.8 us -> none  [shifted(): return lax.ppermute(x, axis, pairs)]
    all_gather x2 -> x0, waiting for transfers between devices: 50.9 us -> none  [the longest x1 36.8 us: per_device(): lax.all_gather(fc2_weight, 'dp', axis=1, tiled=True)]
  transfers between devices with their start and end apart: 35 -> 0, of which waited for: 32 -> 0; matrix products, arithmetic and copies ran while one was open for 6% -> 0% of each run, Pallas kernels for 0% -> 0%
where the time goes in v1:
time: 290 us; the launch traced here: 289 us
  Pallas kernels  265 us (91%)
  local copies, waits for them, and re-layouts  22.7 us (8%)
    pallas_call x1, Pallas kernels, per_device(): pl.pallas_call(functools.partial(kernel, z), out_shape=tuple((o for o, _...  265 us
    unnamed x24, local copies, waits for them, and re-layouts  14.7 us

profile of v1, /device:TPU:0, one launch (start us, length us, event | category | flops | bytes accessed | tf_op | source)
XLA Modules:
  0.0 289.3 jit_solution(1974447543856079595)
XLA Ops:
  0.7 0.8 concatenate.6
  1.4 0.0 copy-start.1
  1.4 0.9 dynamic_update_slice.10
  2.3 1.3 pad.9.refs_7_
  3.7 0.7 constant_dynamic-update-slice_fusion
  4.4 0.2 dynamic_update_slice.9
  4.5 0.6 fusion.4.refs_6_
  5.2 3.5 %copy.32.refs_0_ = bf16[16,98,512]{2,1,0:T(8,128)(2,1)} copy(bf16[16,98,512]{2,0,1:T(8,128)(2,1)} %param.17) | data formatting | bytes 3211264 | tf_op args[0]
  8.7 0.0 copy-done.1
  8.7 2.1 copy.33.refs_1_
  10.8 265.2 %two_blocks.1 = (bf16[16,98,512]{2,1,0:T(8,128)(2,1)}, bf16[16,98,512]{2,1,0:T(8,128)(2,1)}, f32[3,64,256]{2,1,0:T(8,128)}, f32[32,512]{1,0:T(8,128)}, f32[64,10...) custom-call(bf16[16,98,512]{2,1,0:T(8,128)(2,1)} %copy.32.refs_0_, ...), custom_call_target="tpu_custom_call" | custom-call | tf_op jit(solution)/shard_map/two_blocks/pallas_call | solution.py:1058
  276.0 0.0 copy-start
  276.0 3.2 %copy.34 = bf16[1,16,98,512]{3,1,2,0:T(8,128)(2,1)} copy(bf16[1,16,98,512]{3,2,1,0:T(8,128)(2,1)} %bitcast.30) | data formatting | bytes 3211264
  279.3 0.0 copy-done
  279.3 0.0 copy-start.2
  279.3 1.7 copy.35
  281.0 0.8 dynamic-slice_bitcast_fusion
  281.7 0.6 copy.36
  282.3 1.5 constant_dynamic-slice_fusion.2
  283.8 0.7 constant_dynamic-slice_fusion.7
  284.5 0.7 slice_bitcast_fusion
  285.2 0.5 constant_dynamic-slice_fusion
  285.8 0.1 reverse
  285.9 0.7 slice_bitcast_fusion.1
  286.6 0.0 copy-done.4
  286.6 0.7 copy.45
  287.3 0.0 copy-done.5
  287.3 0.6 copy.46
  287.9 0.0 copy-done.3
  287.9 0.7 copy.47
  288.6 0.0 copy-done.2
  288.6 0.7 copy.48
  (10 shorter events, 0.1 us)
Async XLA Ops:
  1.4 7.2 %copy-start.1 = (bf16[16,98,512]{2,0,1:T(8,128)(2,1)S(1)}, bf16[16,98,512]{2,0,1:T(8,128)(2,1)}, u32[]{:S(2)}) copy-start(bf16[16,98,512]{2,0,1:T(8,128)(2,1)} %param.18) | copy-start | bytes 4816900
  276.0 3.3 %copy-start = (bf16[16,98,512]{2,1,0:T(8,128)(2,1)S(1)}, bf16[16,98,512]{2,1,0:T(8,128)(2,1)}, u32[]{:S(2)}) copy-start(bf16[16,98,512]{2,1,0:T(8,128)(2,1)} %get-tuple-element.23) | copy-start | bytes 4816900
  279.3 7.3 %copy-start.4 = (f32[3,64,256]{2,1,0:T(8,128)S(1)}, f32[3,64,256]{2,1,0:T(8,128)}, u32[]{:S(2)}) copy-start(f32[3,64,256]{2,1,0:T(8,128)} %get-tuple-element.25) | copy-start | bytes 589828
  279.3 8.0 %copy-start.5 = (f32[32,512]{1,0:T(8,128)S(1)}, f32[32,512]{1,0:T(8,128)}, u32[]{:S(2)}) copy-start(f32[32,512]{1,0:T(8,128)} %get-tuple-element.26) | copy-start | bytes 196612
  279.3 8.6 %copy-start.3 = (f32[64,1024]{1,0:T(8,128)S(1)}, f32[64,1024]{1,0:T(8,128)}, u32[]{:S(2)}) copy-start(f32[64,1024]{1,0:T(8,128)} %get-tuple-element.27) | copy-start | bytes 786436
  279.3 9.3 %copy-start.2 = (f32[128,512]{1,0:T(8,128)S(1)}, f32[128,512]{1,0:T(8,128)}, u32[]{:S(2)}) copy-start(f32[128,512]{1,0:T(8,128)} %get-tuple-element.28) | copy-start | bytes 786436
